TPU v7x, 128 devices: a whole 4x4x4 slice. The times are simulated.
128 devices in a mesh: depth: 2 (over core), row: 16 (over z, x), col: 4 (over y).
Axes of the slice: x: 4, y: 4, z: 4, core: 2. Of those that a mesh axis runs over, the one named last changes fastest.
Arguments:
- right_side: bfloat16 [4, 16, 8, 128, 512], P(None, 'row', ('depth', 'col')), may hold values from -6 to 6
- inverse_diag: bfloat16 [4, 16, 8, 1, 128, 128], P(None, 'row', ('depth', 'col')), may hold values from -2 to 2.5, as said below
- coupling: bfloat16 [3, 16, 1024, 8, 2048], P(None, 'row', None, ('depth', 'col')), may hold values from -0.0625 to 0.0625
- pattern: int32 [3, 16, 8, 8, 16], P(None, 'row', None, ('depth', 'col')), may hold values 0 or 1
Outputs:
- forward_solution: bfloat16 [4, 16, 8, 128, 512], P(None, 'row', ('depth', 'col'))
- solution: bfloat16 [4, 16, 8, 128, 512], P(None, 'row', ('depth', 'col'))
Inputs may be any that keep to these rules, and one draw needn't show every extreme that they name: `inverse_diag`: each block is lower triangular with positive diagonal.
All inputs are finite; a program needn't handle non-finite values. No bound on the sum of `pattern` on one device may be relied on, other than what follows from the above.
Results may differ from a plain program's by a relative error of at most 0.025.
Values may be sent and summed in bfloat16 or wider, within the bound.
A program may use at most 128 MiB of HBM per device.

v0:
```python
import jax
import jax.numpy as jnp
from jax import lax
from jax.sharding import PartitionSpec as P


def apply_inverse(inverse, vector, transposed):
    blocks_in = vector.reshape(inverse.shape[0], inverse.shape[1], vector.shape[-1])
    einsum_form = "tji,tjn->tin" if transposed else "tij,tjn->tin"
    result = jnp.einsum(einsum_form, inverse, blocks_in, preferred_element_type=jnp.float32)
    return result.astype(jnp.bfloat16).reshape(vector.shape)


def lift_upward(masked, share_in):
    portion = lax.all_gather(share_in, "row", axis=0, tiled=True)
    span_rows = portion.shape[0] * portion.shape[2]
    return jnp.dot(
        masked, portion.reshape(span_rows, portion.shape[-1]), preferred_element_type=jnp.float32
    )


def carry_downward(masked, share_in):
    portion = lax.all_gather(share_in, ("depth", "col"), axis=1, tiled=True)
    span_rows = portion.shape[1] * portion.shape[2]
    return lax.dot_general(
        masked,
        portion.reshape(span_rows, portion.shape[-1]),
        (((0,), (0,)), ((), ())),
        preferred_element_type=jnp.float32,
    )


def forward_sum(partial_value, share_rows):
    blocks = partial_value.reshape(
        lax.axis_size(("depth", "col")), share_rows, partial_value.shape[-1]
    )
    summed = lax.psum(blocks.astype(jnp.bfloat16), ("depth", "col")).astype(jnp.float32)
    return lax.dynamic_index_in_dim(summed, lax.axis_index(("depth", "col")), 0, keepdims=False)


def backward_sum(partial_value, share_rows):
    blocks = partial_value.reshape(lax.axis_size("row"), share_rows, partial_value.shape[-1])
    summed = lax.psum(blocks.astype(jnp.bfloat16), "row").astype(jnp.float32)
    return lax.dynamic_index_in_dim(summed, lax.axis_index("row"), 0, keepdims=False)


def body(right_side, inverse_diag, coupling, pattern):
    levels = right_side.shape[0]
    share_rows = right_side.shape[3]
    rhs_cols = right_side.shape[4]
    block_width = inverse_diag.shape[-1]
    masked = []
    for pair_at in range(levels - 1):
        slab = coupling[pair_at, 0, :, 0, :]
        gate = pattern[pair_at, 0, :, 0, :].astype(jnp.bfloat16)
        shaped = (
            slab.reshape(gate.shape[0], block_width, gate.shape[1], block_width)
            * gate[:, None, :, None]
        )
        masked.append(shaped.reshape(slab.shape))
    panel_spans = [(0, rhs_cols)]
    fwd_levels = []
    for level_at in range(levels):
        pieces = []
        for panel_at, (col_first, col_last) in enumerate(panel_spans):
            source = right_side[level_at, 0, 0, :, col_first:col_last]
            if level_at == 0:
                residual = source
            else:
                partial_value = lift_upward(
                    masked[level_at - 1], fwd_levels[level_at - 1][panel_at][None, None]
                )
                residual = (
                    source.astype(jnp.float32) - forward_sum(partial_value, share_rows)
                ).astype(jnp.bfloat16)
            pieces.append(apply_inverse(inverse_diag[level_at, 0, 0], residual, False))
        fwd_levels.append(pieces)
    bwd_levels = [None] * levels
    for level_at in reversed(range(levels)):
        pieces = []
        panel_at = 0
        known_part = fwd_levels[level_at][panel_at]
        if level_at == levels - 1:
            residual = known_part
        else:
            partial_value = carry_downward(
                masked[level_at], bwd_levels[level_at + 1][panel_at][None, None]
            )
            residual = (
                known_part.astype(jnp.float32) - backward_sum(partial_value, share_rows)
            ).astype(jnp.bfloat16)
        pieces.append(apply_inverse(inverse_diag[level_at, 0, 0], residual, True))
        bwd_levels[level_at] = pieces
    forward_rows = []
    backward_rows = []
    for level_at in range(levels):
        forward_rows.append(jnp.concatenate(fwd_levels[level_at], axis=1))
        backward_rows.append(jnp.concatenate(bwd_levels[level_at], axis=1))
    forward_solution = jnp.stack(forward_rows).reshape(levels, 1, 1, share_rows, rhs_cols)
    solution = jnp.stack(backward_rows).reshape(levels, 1, 1, share_rows, rhs_cols)
    return (forward_solution, solution)


def solution(mesh):
    placed = (
        P(None, "row", ("depth", "col"), None, None),
        P(None, "row", ("depth", "col"), None, None, None),
        P(None, "row", None, ("depth", "col"), None),
        P(None, "row", None, ("depth", "col"), None),
    )
    return jax.shard_map(
        body,
        mesh=mesh,
        in_specs=placed,
        out_specs=(
            P(None, "row", ("depth", "col"), None, None),
            P(None, "row", ("depth", "col"), None, None),
        ),
        check_vma=False,
    )
```

profile of v0, /device:TPU:0, one launch (start us, length us, event | category | flops | bytes accessed | tf_op | source)
XLA Modules:
  0.0 735.9 jit_solution(18099699853977080136)
XLA Ops:
  7.2 0.0 all-gather.13.cloned.1.call-start
  7.2 1.8 convolution_convert_fusion.10
  9.0 0.0 all-gather.13.cloned.1.call-update
  9.0 0.0 all-reduce.7.cloned.1.call-start
  9.0 0.7 convert.11
  9.8 2.6 mul.62
  12.3 7.3 mul.63
  19.6 2.6 mul.71
  22.2 7.3 mul.72
  29.6 2.6 mul.67
  32.2 7.4 mul.68
  39.5 13.6 %slice_multiply_fusion.2 = (bf16[1,1,1024,1,2048]{4,2,3,1,0:T(8,128)(2,1)}, bf16[1,1,1024,1,2048]{4,2,3,1,0:T(8,128)(2,1)}, bf16[1,1,1024,1,2048]{4,2,3,1,0:T(8,128)(2,1)}) fusion(bf16[1,1,1024,1,2048]{4,2,3,1,0:T(8,128)(2,1)} %mul.63, bf16[3,1,1024,1,2048]{4,2,3,1,0:T(8,128)(2,1)} %param.6, bf16[1,1,1024,1,2048]{4,2,3,1,0:T(8,128)(2,1)} %mul.72, ...), kind=kLoop, calls=%fused_computation.8 | loop fusion | flops 6291456 | bytes 37748736 | tf_op jit(solution)/shard_map/mul | solution.py:57
  53.1 5.1 all-gather.13.cloned.1.call-done
  58.2 6.2 fusion.9
  64.5 0.0 all-reduce.7.cloned.1.call-update
  64.5 0.0 all-gather.15.cloned.1.call-start
  64.5 62.1 %all-reduce.7.cloned.1.call-done = bf16[8,128,512]{2,1,0:T(8,128)(2,1)} async-done(((bf16[8,128,512]{2,1,0:T(8,128)(2,1)}), bf16[8,128,512]{2,1,0:T(8,128)(2,1)}) %all-reduce.7.cloned.1.call-update) | async-done | bytes 1048592 | tf_op jit(solution)/shard_map/psum | solution.py:37
  126.6 1.7 convolution_convert_fusion.5
  128.4 0.0 all-gather.15.cloned.1.call-update
  128.4 0.0 all-reduce.9.cloned.1.call-start
  128.5 45.3 %all-gather.15.cloned.1.call-done = bf16[2048,512]{1,0:T(8,128)(2,1)} async-done(((bf16[128,512]{1,0:T(8,128)(2,1)}), bf16[2048,512]{1,0:T(8,128)(2,1)}) %all-gather.15.cloned.1.call-update) | async-done | bytes 2097168 | tf_op jit(solution)/shard_map/all_gather | solution.py:15
  173.7 6.2 fusion.12
  179.9 0.0 all-reduce.9.cloned.1.call-update
  180.0 0.0 all-gather.17.cloned.1.call-start
  180.0 62.1 %all-reduce.9.cloned.1.call-done = bf16[8,128,512]{2,1,0:T(8,128)(2,1)} async-done(((bf16[8,128,512]{2,1,0:T(8,128)(2,1)}), bf16[8,128,512]{2,1,0:T(8,128)(2,1)}) %all-reduce.9.cloned.1.call-update) | async-done | bytes 1048592 | tf_op jit(solution)/shard_map/psum | solution.py:37
  242.1 1.7 convolution_convert_fusion.4
  243.9 0.0 all-gather.17.cloned.1.call-update
  243.9 0.0 all-reduce.11.cloned.1.call-start
  243.9 44.5 %all-gather.17.cloned.1.call-done = bf16[2048,512]{1,0:T(8,128)(2,1)} async-done(((bf16[128,512]{1,0:T(8,128)(2,1)}), bf16[2048,512]{1,0:T(8,128)(2,1)}) %all-gather.17.cloned.1.call-update) | async-done | bytes 2097168 | tf_op jit(solution)/shard_map/all_gather | solution.py:15
  288.5 6.2 fusion.15
  294.7 0.0 all-reduce.11.cloned.1.call-update
  294.7 0.0 all-gather.19.cloned.1.call-start
  294.7 62.1 %all-reduce.11.cloned.1.call-done = bf16[8,128,512]{2,1,0:T(8,128)(2,1)} async-done(((bf16[8,128,512]{2,1,0:T(8,128)(2,1)}), bf16[8,128,512]{2,1,0:T(8,128)(2,1)}) %all-reduce.11.cloned.1.call-update) | async-done | bytes 1048592 | tf_op jit(solution)/shard_map/psum | solution.py:37
  356.8 1.1 convolution_convert_fusion.3
  357.9 0.9 convolution_convert_fusion.9
  358.8 0.0 all-gather.19.cloned.1.call-update
  358.8 0.2 all-reduce.13.cloned.1.call-start
  359.0 15.1 %fusion.2 = (bf16[2048,1024]{0,1:T(8,128)(2,1)}, bf16[2048,1024]{0,1:T(8,128)(2,1)}, bf16[2048,1024]{0,1:T(8,128)(2,1)}) fusion(bf16[128,8,16,128]{3,2,1,0:T(8,128)(2,1)} %bitcast.180, bf16[3,1,1024,1,2048]{4,2,3,1,0:T(8,128)(2,1)} %param.6, bf16[128,8,16,128]{3,2,1,0:T(8,128)(2,1)} %bitcast.182, bf16[128,8,16,128]{3,2,1,0:T(8,128)(2,1)} %bitcast.181), kind=kLoop, calls=%fused_computation.5 | loop fusion | flops 6291456 | bytes 37748736 | tf_op jit(solution)/shard_map/dot_general | solution.py:25
  374.1 6.4 copy.26
  380.5 1.1 all-gather.19.cloned.1.call-done
  381.6 6.3 convolution_convert_fusion.2
  387.9 0.0 all-reduce.13.cloned.1.call-update
  387.9 0.0 all-gather.21.cloned.1.call-start
  387.9 92.3 %all-reduce.13.cloned.1.call-done = bf16[16,128,512]{2,1,0:T(8,128)(2,1)} async-done(((bf16[16,128,512]{2,1,0:T(8,128)(2,1)}), bf16[16,128,512]{2,1,0:T(8,128)(2,1)}) %all-reduce.13.cloned.1.call-update) | async-done | bytes 2097168 | tf_op jit(solution)/shard_map/psum | solution.py:43
  480.2 1.8 convolution_convert_fusion.8
  482.0 0.0 all-gather.21.cloned.1.call-update
  482.0 0.0 all-reduce.15.cloned.1.call-start
  482.1 6.4 copy.25
  488.5 16.4 %all-gather.21.cloned.1.call-done = bf16[1024,512]{0,1:T(8,128)(2,1)} async-done(((bf16[128,512]{0,1:T(8,128)(2,1)}), bf16[1024,512]{0,1:T(8,128)(2,1)}) %all-gather.21.cloned.1.call-update) | async-done | bytes 1048592 | tf_op jit(solution)/shard_map/all_gather | solution.py:23
  504.9 6.3 convolution_convert_fusion.1
  511.2 0.0 all-reduce.15.cloned.1.call-update
  511.2 0.0 all-gather.23.cloned.1.call-start
  511.2 92.3 %all-reduce.15.cloned.1.call-done = bf16[16,128,512]{2,1,0:T(8,128)(2,1)} async-done(((bf16[16,128,512]{2,1,0:T(8,128)(2,1)}), bf16[16,128,512]{2,1,0:T(8,128)(2,1)}) %all-reduce.15.cloned.1.call-update) | async-done | bytes 2097168 | tf_op jit(solution)/shard_map/psum | solution.py:43
  603.5 1.8 convolution_convert_fusion.7
  605.3 0.0 all-gather.23.cloned.1.call-update
  605.3 0.0 all-reduce.17.cloned.1.call-start
  605.3 6.4 copy.24
  611.7 16.4 %all-gather.23.cloned.1.call-done = bf16[1024,512]{0,1:T(8,128)(2,1)} async-done(((bf16[128,512]{0,1:T(8,128)(2,1)}), bf16[1024,512]{0,1:T(8,128)(2,1)}) %all-gather.23.cloned.1.call-update) | async-done | bytes 1048592 | tf_op jit(solution)/shard_map/all_gather | solution.py:23
  628.2 6.3 convolution_convert_fusion
  634.5 0.9 maximum_bitcast_fusion
  635.3 91.5 %all-reduce.17.cloned.1.call-done = bf16[16,128,512]{2,1,0:T(8,128)(2,1)} async-done(((bf16[16,128,512]{2,1,0:T(8,128)(2,1)}), bf16[16,128,512]{2,1,0:T(8,128)(2,1)}) %all-reduce.17.cloned.1.call-update) | async-done | bytes 2097168 | tf_op jit(solution)/shard_map/psum | solution.py:43
  726.8 1.1 fusion.18
  728.0 0.1 maximum_bitcast_fusion.1
  728.1 1.0 copy.17
  (18 shorter events, 0.1 us)
Async XLA Ops:
  7.2 51.1 %all-gather.13.cloned.1.call-start = ((), (), s32[]{:S(2)}) async-start(), calls=%async_computation.6 | async-start | bytes 2228224 | tf_op jit(solution)/shard_map/all_gather | solution.py:15
  9.0 117.6 %all-reduce.7.cloned.1.call-start = ((), (), s32[]{:S(2)}) async-start(), calls=%async_computation | async-start | bytes 2097152 | tf_op jit(solution)/shard_map/psum | solution.py:37
  58.2 68.4 %copy-start.6 = (bf16[4,1,1,128,512]{4,3,2,1,0:T(8,128)(2,1)S(1)}, bf16[4,1,1,128,512]{4,3,2,1,0:T(8,128)(2,1)}, u32[]{:S(2)}) copy-start(bf16[4,1,1,128,512]{4,3,2,1,0:T(8,128)(2,1)} %param.4) | copy-start | bytes 1572868
  58.2 68.4 %copy-start.7 = (bf16[4,1,1,1,128,128]{5,4,3,2,1,0:T(8,128)(2,1)S(1)}, bf16[4,1,1,1,128,128]{5,4,3,2,1,0:T(8,128)(2,1)}, u32[]{:S(2)}) copy-start(bf16[4,1,1,1,128,128]{5,4,3,2,1,0:T(8,128)(2,1)} %param.5) | copy-start | bytes 393220
  64.5 109.2 %all-gather.15.cloned.1.call-start = ((), (), s32[]{:S(2)}) async-start(), calls=%async_computation.7 | async-start | bytes 2228224 | tf_op jit(solution)/shard_map/all_gather | solution.py:15
  128.4 113.7 %all-reduce.9.cloned.1.call-start = ((), (), s32[]{:S(2)}) async-start(), calls=%async_computation.1 | async-start | bytes 2097152 | tf_op jit(solution)/shard_map/psum | solution.py:37
  180.0 108.5 %all-gather.17.cloned.1.call-start = ((), (), s32[]{:S(2)}) async-start(), calls=%async_computation.8 | async-start | bytes 2228224 | tf_op jit(solution)/shard_map/all_gather | solution.py:15
  243.9 113.0 %all-reduce.11.cloned.1.call-start = ((), (), s32[]{:S(2)}) async-start(), calls=%async_computation.2 | async-start | bytes 2097152 | tf_op jit(solution)/shard_map/psum | solution.py:37
  294.7 86.9 %all-gather.19.cloned.1.call-start = ((), (), s32[]{:S(2)}) async-start(), calls=%async_computation.9 | async-start | bytes 1179648 | tf_op jit(solution)/shard_map/all_gather | solution.py:23
  358.8 121.4 %all-reduce.13.cloned.1.call-start = ((), (), s32[]{:S(2)}) async-start(), calls=%async_computation.3 | async-start | bytes 4194304 | tf_op jit(solution)/shard_map/psum | solution.py:43
  381.6 98.7 %copy-start.2 = (bf16[512,128]{0,1:T(8,128)(2,1)S(1)}, bf16[512,128]{0,1:T(8,128)(2,1)}, u32[]{:S(2)}) copy-start(bf16[512,128]{0,1:T(8,128)(2,1)} %convolution_convert_fusion.4) | copy-start | bytes 393220
  387.9 117.0 %all-gather.21.cloned.1.call-start = ((), (), s32[]{:S(2)}) async-start(), calls=%async_computation.10 | async-start | bytes 1179648 | tf_op jit(solution)/shard_map/all_gather | solution.py:23
  482.0 121.4 %all-reduce.15.cloned.1.call-start = ((), (), s32[]{:S(2)}) async-start(), calls=%async_computation.4 | async-start | bytes 4194304 | tf_op jit(solution)/shard_map/psum | solution.py:43
  504.9 98.6 %copy-start.1 = (bf16[512,128]{0,1:T(8,128)(2,1)S(1)}, bf16[512,128]{0,1:T(8,128)(2,1)}, u32[]{:S(2)}) copy-start(bf16[512,128]{0,1:T(8,128)(2,1)} %convolution_convert_fusion.5) | copy-start | bytes 393220
  511.2 117.0 %all-gather.23.cloned.1.call-start = ((), (), s32[]{:S(2)}) async-start(), calls=%async_computation.11 | async-start | bytes 1179648 | tf_op jit(solution)/shard_map/all_gather | solution.py:23
  605.3 121.5 %all-reduce.17.cloned.1.call-start = ((), (), s32[]{:S(2)}) async-start(), calls=%async_computation.5 | async-start | bytes 4194304 | tf_op jit(solution)/shard_map/psum | solution.py:43
  628.1 6.3 copy-start
  628.1 99.8 %copy-start.3 = (bf16[512,128]{1,0:T(8,128)(2,1)S(1)}, bf16[512,128]{1,0:T(8,128)(2,1)}, u32[]{:S(2)}) copy-start(bf16[512,128]{1,0:T(8,128)(2,1)} %convolution_convert_fusion.9) | copy-start | bytes 393220
  628.1 99.8 %copy-start.4 = (bf16[512,128]{1,0:T(8,128)(2,1)S(1)}, bf16[512,128]{1,0:T(8,128)(2,1)}, u32[]{:S(2)}) copy-start(bf16[512,128]{1,0:T(8,128)(2,1)} %convolution_convert_fusion.8) | copy-start | bytes 393220
  628.2 99.8 %copy-start.5 = (bf16[512,128]{1,0:T(8,128)(2,1)S(1)}, bf16[512,128]{1,0:T(8,128)(2,1)}, u32[]{:S(2)}) copy-start(bf16[512,128]{1,0:T(8,128)(2,1)} %convolution_convert_fusion.7) | copy-start | bytes 393220
Sparse Core Ops, SparseCore 0:
  10.7 47.4 all-gather.12
  64.6 61.9 all-reduce.6
  129.4 44.3 all-gather.14
  180.1 61.9 all-reduce.8
  244.1 44.3 all-gather.16
  294.8 61.9 all-reduce.10
  358.9 22.6 all-gather.18
  388.0 92.1 all-reduce.12
  482.2 22.6 all-gather.20
  511.3 92.1 all-reduce.14
  605.4 22.6 all-gather.22
  634.6 92.1 all-reduce.16
where the time goes:
time: 737 us; the launch traced here: 736 us
  waiting for transfers between devices  591 us (80%)
  local copies, waits for them, and re-layouts  50 us (7%)
  matrix products  49.3 us (7%)
  other arithmetic  30.3 us (4%)
  between operations  14.3 us (2%)
    psum x3, waiting for transfers between devices, backward_sum(): summed = lax.psum(blocks.astype(jnp.bfloat16), 'row').astype(jnp.float32)  276 us
    psum x3, waiting for transfers between devices, forward_sum(): lax.psum(blocks.astype(jnp.bfloat16), ('depth', 'col')).astype(jnp.float32)  186 us
    all_gather x3, waiting for transfers between devices, lift_upward(): portion = lax.all_gather(share_in, 'row', axis=0, tiled=True)  94.9 us
    all_gather x3, waiting for transfers between devices, carry_downward(): portion = lax.all_gather(share_in, ('depth', 'col'), axis=1, tiled=True)  33.9 us
    mul x6, local copies, waits for them, and re-layouts, body(): slab.reshape(gate.shape[0], block_width, gate.shape[1], block_width)  29.7 us
    dot_general x3, local copies, waits for them, and re-layouts, carry_downward(): lax.dot_general(masked, portion.reshape(span_rows, portion.shape[-1]), ((...  19.2 us
    dot_general x3, matrix products, carry_downward(): lax.dot_general(masked, portion.reshape(span_rows, portion.shape[-1]), ((...  18.8 us
    dot_general x3, matrix products, lift_upward(): jnp.dot(masked, portion.reshape(span_rows, portion.shape[-1]), preferred_...  18.6 us
  transfers between devices with their start and end apart: 12, of which 12 were waited for; matrix products, arithmetic and copies ran while one was open for 11% of the time, Pallas kernels for 0%

commit v1 on v0

v1 whole, which is shorter than its diff:
```python
import functools

import jax
import jax.numpy as jnp
from jax import lax
from jax.experimental import pallas as pl
from jax.experimental.pallas import tpu as pltpu
from jax.sharding import PartitionSpec as P

F32 = jnp.float32
BF16 = jnp.bfloat16
W = 128
H = 64
PANELS = 4


def kernel(
    nz, nx, ny, levels,
    b_ref, d_ref, gate_ref, m_hbm,
    f_ref, z_ref,
    mv, xg, ps, pr, own, owny, ys, yr, yg, rs, rr0, rr1, ls, lr, ownb, ft,
    load_sem, send_sem, recv_sem,
):
    pairs = levels - 1
    items = pairs * PANELS
    dd = lax.axis_index("depth")
    rw = lax.axis_index("row")
    yy = lax.axis_index("col")
    zz = rw // nx
    xx = rw % nx

    def x_peer(step):
        return {"row": zz * nx + (xx + step) % nx}

    def z_peer(step):
        return {"row": ((zz + step) % nz) * nx + xx}

    def y_peer(step):
        return {"col": (yy + step) % ny}

    partner = {"depth": 1 - dd}
    peers = (
        [x_peer(k) for k in range(1, nx)]
        + [z_peer(k) for k in range(1, nz)]
        + [y_peer(k) for k in range(1, ny)]
        + [partner]
    )

    for lv in range(pairs):
        pltpu.make_async_copy(m_hbm.at[lv], mv.at[lv], load_sem.at[lv]).start()

    barrier = pltpu.get_barrier_semaphore()
    for peer in peers:
        pl.semaphore_signal(
            barrier, inc=1, device_id=peer, device_id_type=pl.DeviceIdType.MESH
        )
    pl.semaphore_wait(barrier, len(peers))

    def send(src, dst, stage, item, peer):
        pltpu.make_async_remote_copy(
            src_ref=src,
            dst_ref=dst,
            send_sem=send_sem.at[stage, item],
            recv_sem=recv_sem.at[stage, item],
            device_id=peer,
            device_id_type=pl.DeviceIdType.MESH,
        ).start()

    def total(stage, item):
        return (
            xg.at[item, 0, 0 : nx - 1],
            xg.at[item, 0 : nz - 1],
            pr.at[item],
            yr.at[item],
            yr.at[item],
            pr.at[item],
            xg.at[item, 0 : nz - 1],
            xg.at[item, 0, 0 : nx - 1],
        )[stage]

    def arrived(stage, item):
        ref = total(stage, item)
        pltpu.make_async_copy(ref, ref, recv_sem.at[stage, item]).wait()

    def sent(stage, item):
        ref = total(stage, item)
        pltpu.make_async_copy(ref, ref, send_sem.at[stage, item]).wait()

    def columns(panel):
        return pl.ds(pl.multiple_of(panel * W, W), W)

    def f1(item):
        lv, pn = item // PANELS, item % PANELS
        prev = item - PANELS

        def finish(residual):
            value = jnp.dot(d_ref[lv], residual, preferred_element_type=F32).astype(BF16)
            f_ref[lv, :, columns(pn)] = value

            @pl.when(lv < pairs)
            def _():
                xg[item, zz, xx] = value
                for k in range(1, nx):
                    here = xg.at[item, zz, xx, 0:H]
                    send(here, here, 0, item, x_peer(k))
                for k in range(1, nz):
                    here = xg.at[item, zz, xx, H:W]
                    send(here, here, 0, item, z_peer(k))

            ft[item] = value.astype(F32).T.astype(BF16)

        @pl.when(lv == 0)
        def _():
            finish(b_ref[0, :, columns(pn)])

        @pl.when(lv > 0)
        def _():
            arrived(3, prev)
            acc = owny[pn]
            for k in range(ny - 1):
                acc = acc + yr[prev, k].astype(F32)
            finish((b_ref[lv, :, columns(pn)].astype(F32) - acc).astype(BF16))

    def f2(item):
        arrived(0, item)
        for k in range(1, nz):
            here = xg.at[item, zz, :, 0:H]
            send(here, here, 1, item, z_peer(k))
        for k in range(1, nx):
            here = xg.at[item, :, xx, H:W]
            send(here, here, 1, item, x_peer(k))

    def f3(item):
        lv, pn = item // PANELS, item % PANELS
        arrived(1, item)
        far = pl.ds(pl.multiple_of((1 - dd) * (ny * W), ny * W), ny * W)
        near = pl.ds(pl.multiple_of(dd * (ny * W), ny * W), ny * W)
        gathered = xg[item].reshape(nz * nx * W, W)
        part = jnp.dot(mv[lv, far, :], gathered, preferred_element_type=F32)
        ps[item] = part.astype(BF16).reshape(ny, W, W)
        send(ps.at[item], pr.at[item], 2, item, partner)
        part = jnp.dot(mv[lv, near, :], gathered, preferred_element_type=F32)
        own[pn] = part.reshape(ny, W, W)

    def f4(item):
        pn = item % PANELS
        arrived(2, item)
        for k in range(1, ny):
            at = (yy + k) % ny
            ys[item, k - 1] = (own[pn, at] + pr[item, at].astype(F32)).astype(BF16)
            send(ys.at[item, k - 1], yr.at[item, k - 1], 3, item, y_peer(k))
        owny[pn] = own[pn, yy] + pr[item, yy].astype(F32)

    def b1(item):
        step, pn = item // PANELS, item % PANELS
        lv = levels - 1 - step
        prev = item - PANELS

        def finish(residual):
            value = jnp.dot(residual, d_ref[lv], preferred_element_type=F32).astype(BF16)

            @pl.when(step < pairs)
            def _():
                mine = dd * ny + yy
                yg[item, mine] = value
                for k in range(1, ny):
                    here = yg.at[item, mine]
                    send(here, here, 4, item, y_peer(k))

            z_ref[lv, :, columns(pn)] = value.astype(F32).T.astype(BF16)

        @pl.when(step == 0)
        def _():
            finish(ft[lv * PANELS + pn])

        @pl.when(step > 0)
        def _():
            arrived(7, prev)
            acc0 = ownb[pn, 0:H]
            for k in range(nx - 1):
                acc0 = acc0 + lr[prev, 0, k].astype(F32)
            acc1 = ownb[pn, H:W]
            for k in range(nz - 1):
                acc1 = acc1 + lr[prev, 1, k].astype(F32)
            acc = jnp.concatenate([acc0, acc1], axis=0)
            finish((ft[lv * PANELS + pn].astype(F32) - acc).astype(BF16))

    def b2(item):
        arrived(4, item)
        here = yg.at[item, pl.ds(dd * ny, ny)]
        send(here, here, 5, item, partner)

    def b3(item):
        lv = pairs - 1 - item // PANELS
        arrived(5, item)
        solved = jnp.concatenate([yg[item, k] for k in range(2 * ny)], axis=1)
        for k in range(1, nz + 1):
            at = (zz + k) % nz
            span = pl.ds(pl.multiple_of(at * (nx * W), nx * W), nx * W)
            part = jnp.dot(solved, mv[lv, :, span], preferred_element_type=F32).astype(BF16)
            for j in range(nx):
                rs[item, at, j] = part[:, j * W : (j + 1) * W]
            if k < nz:
                send(rs.at[item, at, :, 0:H], rr0.at[item, k - 1], 6, item, z_peer(k))
        for k in range(1, nx):
            at = (xx + k) % nx
            send(rs.at[item, :, at, H:W], rr1.at[item, k - 1], 6, item, x_peer(k))

    def b4(item):
        pn = item % PANELS
        arrived(6, item)
        for k in range(nx):
            at = (xx + k) % nx
            acc = rs[item, zz, at, 0:H].astype(F32)
            for j in range(nz - 1):
                acc = acc + rr0[item, j, at].astype(F32)
            if k == 0:
                ownb[pn, 0:H] = acc
            else:
                ls[item, 0, k - 1] = acc.astype(BF16)
                send(ls.at[item, 0, k - 1], lr.at[item, 0, k - 1], 7, item, x_peer(k))
        for k in range(nz):
            at = (zz + k) % nz
            acc = rs[item, at, xx, H:W].astype(F32)
            for j in range(nx - 1):
                acc = acc + rr1[item, j, at].astype(F32)
            if k == 0:
                ownb[pn, H:W] = acc
            else:
                ls[item, 1, k - 1] = acc.astype(BF16)
                send(ls.at[item, 1, k - 1], lr.at[item, 1, k - 1], 7, item, z_peer(k))

    def mask(lv):
        pltpu.make_async_copy(m_hbm.at[lv], mv.at[lv], load_sem.at[lv]).wait()

        def rows(t, carry):
            span = pl.ds(pl.multiple_of(t * W, W), W)
            gate = gate_ref[lv * (2 * ny) + t].astype(BF16)
            mv[lv, span, :] = mv[lv, span, :] * gate
            return carry

        lax.fori_loop(0, 2 * ny, rows, 0)

    def stage(fn, index, count):
        @pl.when((index >= 0) & (index < count))
        def _():
            fn(index)

    def slot(s, carry):
        j = s - items
        stage(f1, s, items + PANELS)
        stage(f4, s - 3, items)
        stage(f2, s - 1, items)
        stage(f3, s - 2, items)

        @pl.when((s % PANELS == 1) & (s < items))
        def _():
            mask(s // PANELS)

        stage(b2, j - 1, items)
        stage(b1, j, items + PANELS)
        stage(b4, j - 3, items)
        stage(b3, j - 1, items)
        return carry

    lax.fori_loop(0, 2 * items + PANELS, slot, 0)

    def drain(item, carry):
        for st in range(8):
            sent(st, item)
        return carry

    lax.fori_loop(0, items, drain, 0)


def body(nz, nx, ny, right_side, inverse_diag, coupling, pattern):
    levels, rhs = right_side.shape[0], right_side.shape[4]
    pairs = levels - 1
    items = pairs * PANELS
    rows, cols = coupling.shape[2], coupling.shape[4]
    b = right_side.reshape(levels, W, rhs)
    d = inverse_diag.reshape(levels, W, W)
    m = coupling.reshape(pairs, rows, cols)
    gate = jnp.repeat(
        pattern.reshape(pairs * 2 * ny, 1, nz * nx).astype(F32), W, axis=2
    )
    vm = pl.BlockSpec(memory_space=pltpu.VMEM)
    f, z = pl.pallas_call(
        functools.partial(kernel, nz, nx, ny, levels),
        out_shape=[jax.ShapeDtypeStruct((levels, W, rhs), BF16)] * 2,
        in_specs=[vm, vm, vm, pl.BlockSpec(memory_space=pl.ANY)],
        out_specs=[vm, vm],
        scratch_shapes=[
            pltpu.VMEM((pairs, rows, cols), BF16),
            pltpu.VMEM((items, nz, nx, W, W), BF16),
            pltpu.VMEM((items, ny, W, W), BF16),
            pltpu.VMEM((items, ny, W, W), BF16),
            pltpu.VMEM((PANELS, ny, W, W), F32),
            pltpu.VMEM((PANELS, W, W), F32),
            pltpu.VMEM((items, ny - 1, W, W), BF16),
            pltpu.VMEM((items, ny - 1, W, W), BF16),
            pltpu.VMEM((items, 2 * ny, W, W), BF16),
            pltpu.VMEM((items, nz, nx, W, W), BF16),
            pltpu.VMEM((items, nz - 1, nx, H, W), BF16),
            pltpu.VMEM((items, nx - 1, nz, H, W), BF16),
            pltpu.VMEM((items, 2, nx - 1, H, W), BF16),
            pltpu.VMEM((items, 2, nx - 1, H, W), BF16),
            pltpu.VMEM((PANELS, W, W), F32),
            pltpu.VMEM((items + PANELS, W, W), BF16),
            pltpu.SemaphoreType.DMA((pairs,)),
            pltpu.SemaphoreType.DMA((8, items)),
            pltpu.SemaphoreType.DMA((8, items)),
        ],
        compiler_params=pltpu.CompilerParams(
            collective_id=0, has_side_effects=True, vmem_limit_bytes=60 * 1024 * 1024
        ),
    )(b, d, gate, m)
    shape = right_side.shape
    return f.reshape(shape), z.reshape(shape)


def solution(mesh):
    placed = (
        P(None, "row", ("depth", "col"), None, None),
        P(None, "row", ("depth", "col"), None, None, None),
        P(None, "row", None, ("depth", "col"), None),
        P(None, "row", None, ("depth", "col"), None),
    )
    side = round(mesh.shape["row"] ** 0.5)
    return jax.shard_map(
        functools.partial(body, side, side, mesh.shape["col"]),
        mesh=mesh,
        in_specs=placed,
        out_specs=(placed[0], placed[0]),
        check_vma=False,
    )
```

time: 737 us -> 136 us (0.18)
  waiting for transfers between devices: 591 us -> 0 us
  Pallas kernels: 0 us -> 130 us
  matrix products: 49.3 us -> 0 us
  local copies, waits for them, and re-layouts: 50 us -> 4.53 us
  other arithmetic: 30.3 us -> 0.72 us
  between operations: 14.3 us -> 0.64 us
    psum x6 -> x0, waiting for transfers between devices: 462 us -> none  [the longest x3 276 us: backward_sum(): summed = lax.psum(blocks.astype(jnp.bfloat16), 'row').astype(jnp.float32)]
    pallas_call x0 -> x1, Pallas kernels: none -> 130 us  [body(): pl.pallas_call(functools.partial(kernel, nz, nx, ny, levels), out_shape=[...]
    all_gather x6 -> x0, waiting for transfers between devices: 129 us -> none  [the longest x3 94.9 us: lift_upward(): portion = lax.all_gather(share_in, 'row', axis=0, tiled=True)]
    dot_general x14 -> x0, matrix products: 49.3 us -> none  [the longest x3 18.8 us: carry_downward(): lax.dot_general(masked, portion.reshape(span_rows, portion.shape[-1]), ((...]
    mul x6 -> x0, local copies, waits for them, and re-layouts: 29.7 us -> none  [body(): slab.reshape(gate.shape[0], block_width, gate.shape[1], block_width)]
    dot_general x3 -> x0, local copies, waits for them, and re-layouts: 19.2 us -> none  [carry_downward(): lax.dot_general(masked, portion.reshape(span_rows, portion.shape[-1]), ((...]
    dot_general x1 -> x0, other arithmetic: 15.1 us -> none  [carry_downward(): lax.dot_general(masked, portion.reshape(span_rows, portion.shape[-1]), ((...]
    mul x1 -> x0, other arithmetic: 13.6 us -> none  [body(): slab.reshape(gate.shape[0], block_width, gate.shape[1], block_width)]
  transfers between devices with their start and end apart: 12 -> 0, of which waited for: 12 -> 0; matrix products, arithmetic and copies ran while one was open for 11% -> 0% of each run, Pallas kernels for 0% -> 0%
where the time goes in v1:
time: 136 us
  Pallas kernels  130 us (96%)
  local copies, waits for them, and re-layouts  4.53 us (3%)
    pallas_call x1, Pallas kernels, body(): pl.pallas_call(functools.partial(kernel, nz, nx, ny, levels), out_shape=[...  130 us
    unnamed x2, local copies, waits for them, and re-layouts  3.74 us

profile of v1, /device:TPU:0, one launch (start us, length us, event | category | flops | bytes accessed | tf_op | source)
XLA Modules:
  0.0 135.9 jit_solution(7648755680993583713)
XLA Ops:
  0.6 0.7 convert_element_type.9
  1.3 0.8 broadcast_in_dim.5
  2.1 130.0 %shard_map.59 = (bf16[4,128,512]{2,1,0:T(8,128)(2,1)}, bf16[4,128,512]{2,1,0:T(8,128)(2,1)}) custom-call(bf16[4,128,512]{2,1,0:T(8,128)(2,1)} %bitcast.13, bf16[4,128,128]{2,1,0:T(8,128)(2,1)} %bitcast.16, f32[24,1,2048]{2,1,0:T(1,128)} %bitcast.12, bf16[3,1024,2048]{2,1,0:T(8,128)(2,1)} %bitcast.11), custom_call_target="tpu_custom_call" | custom-call | tf_op jit(solution)/shard_map/pallas_call | solution.py:288
  132.1 1.9 %copy.10 = bf16[4,1,1,128,512]{4,3,2,1,0:T(8,128)(2,1)} copy(bf16[4,1,1,128,512]{4,3,2,1,0:T(8,128)(2,1)} %bitcast.15) | data formatting | bytes 1048576
  134.0 1.9 %copy.11 = bf16[4,1,1,128,512]{4,3,2,1,0:T(8,128)(2,1)} copy(bf16[4,1,1,128,512]{4,3,2,1,0:T(8,128)(2,1)} %bitcast.14) | data formatting | bytes 1048576

commit v2 on v1

v2 whole, which is shorter than its diff:
```python
import functools

import jax
import jax.numpy as jnp
from jax import lax
from jax.experimental import pallas as pl
from jax.experimental.pallas import tpu as pltpu
from jax.sharding import PartitionSpec as P

F32 = jnp.float32
BF16 = jnp.bfloat16
W = 128
H = 64
PANELS = 4


def far_first(n):
    return sorted(range(1, n), key=lambda k: -min(k, n - k))


def kernel(
    nz, nx, ny, levels,
    b_hbm, d_hbm, pat_ref, m_hbm,
    f_hbm, z_hbm,
    bv, dv, fo, zo, mv, xg, ownf, ys, yr, yg, rs, rr0, rr1, ls, lr, ownb, ft,
    load_sem, in_sem, out_sem, send_sem, recv_sem,
):
    pairs = levels - 1
    items = pairs * PANELS
    dd = lax.axis_index("depth")
    rw = lax.axis_index("row")
    yy = lax.axis_index("col")
    zz = rw // nx
    xx = rw % nx
    shares = [(flip, k) for k in far_first(ny) for flip in (0, 1)] + [(1, 0)]

    def x_peer(step):
        return {"row": zz * nx + (xx + step) % nx}

    def z_peer(step):
        return {"row": ((zz + step) % nz) * nx + xx}

    def share_peer(flip, step):
        return {"depth": (dd + flip) % 2, "col": (yy + step) % ny}

    peers = (
        [x_peer(k) for k in range(1, nx)]
        + [z_peer(k) for k in range(1, nz)]
        + [share_peer(*share) for share in shares]
    )

    barrier = pltpu.get_barrier_semaphore()
    for peer in peers:
        pl.semaphore_signal(
            barrier, inc=1, device_id=peer, device_id_type=pl.DeviceIdType.MESH
        )

    def load_inputs(lv):
        return (
            pltpu.make_async_copy(b_hbm.at[lv], bv.at[lv], in_sem.at[0, lv]),
            pltpu.make_async_copy(d_hbm.at[lv], dv.at[lv], in_sem.at[1, lv]),
        )

    for lv in range(levels):
        for copy in load_inputs(lv):
            copy.start()
        if lv < pairs:
            pltpu.make_async_copy(m_hbm.at[lv], mv.at[lv], load_sem.at[lv]).start()

    for copy in load_inputs(0):
        copy.wait()
    pl.semaphore_wait(barrier, len(peers))

    def send(src, dst, stage, item, peer):
        pltpu.make_async_remote_copy(
            src_ref=src,
            dst_ref=dst,
            send_sem=send_sem.at[stage, item],
            recv_sem=recv_sem.at[stage, item],
            device_id=peer,
            device_id_type=pl.DeviceIdType.MESH,
        ).start()

    def total(stage, item):
        return (
            xg.at[item, 0, 0 : nx - 1],
            xg.at[item, 0 : nz - 1],
            yr.at[item],
            yr.at[item],
            xg.at[item, 0 : nz - 1],
            xg.at[item, 0, 0 : nx - 1],
        )[stage]

    def arrived(stage, item):
        ref = total(stage, item)
        pltpu.make_async_copy(ref, ref, recv_sem.at[stage, item]).wait()

    def sent(stage, item):
        ref = total(stage, item)
        pltpu.make_async_copy(ref, ref, send_sem.at[stage, item]).wait()

    def columns(panel):
        return pl.ds(pl.multiple_of(panel * W, W), W)

    def output(hbm, buf, which, lv):
        return pltpu.make_async_copy(buf.at[lv], hbm.at[lv], out_sem.at[which, lv])

    def f1(item):
        lv, pn = item // PANELS, item % PANELS
        prev = item - PANELS

        def finish(residual):
            value = jnp.dot(dv[lv], residual, preferred_element_type=F32).astype(BF16)

            @pl.when(lv < pairs)
            def _():
                xg[item, zz, xx] = value
                for k in far_first(nx):
                    here = xg.at[item, zz, xx, 0:H]
                    send(here, here, 0, item, x_peer(k))
                for k in far_first(nz):
                    here = xg.at[item, zz, xx, H:W]
                    send(here, here, 0, item, z_peer(k))

            fo[lv, :, columns(pn)] = value
            ft[item] = value.astype(F32).T.astype(BF16)

            @pl.when(pn == PANELS - 1)
            def _():
                output(f_hbm, fo, 0, lv).start()

        @pl.when(lv == 0)
        def _():
            finish(bv[0, :, columns(pn)])

        @pl.when(lv > 0)
        def _():
            arrived(2, prev)
            acc = ownf[pn]
            for k in range(2 * ny - 1):
                acc = acc + yr[prev, k].astype(F32)
            finish((bv[lv, :, columns(pn)].astype(F32) - acc).astype(BF16))

    def f2(item):
        arrived(0, item)
        for k in far_first(nz):
            here = xg.at[item, zz, :, 0:H]
            send(here, here, 1, item, z_peer(k))
        for k in far_first(nx):
            here = xg.at[item, :, xx, H:W]
            send(here, here, 1, item, x_peer(k))

    def f3(item):
        lv, pn = item // PANELS, item % PANELS
        arrived(1, item)
        gathered = xg[item].reshape(nz * nx * W, W)
        for k in far_first(ny) + [0]:
            at = (yy + k) % ny
            rows = [
                mv[lv, pl.ds(pl.multiple_of((side * ny + at) * W, W), W), :]
                for side in (dd, (dd + 1) % 2)
            ]
            part = jnp.dot(
                jnp.concatenate(rows, axis=0), gathered, preferred_element_type=F32
            )
            for flip in (0, 1):
                block = part[flip * W : (flip + 1) * W]
                if flip == 0 and k == 0:
                    ownf[pn] = block
                else:
                    slot = flip * ny + k - 1
                    ys[item, slot] = block.astype(BF16)
                    send(ys.at[item, slot], yr.at[item, slot], 2, item, share_peer(flip, k))

    def b1(item):
        step, pn = item // PANELS, item % PANELS
        lv = levels - 1 - step
        prev = item - PANELS

        def finish(residual):
            value = jnp.dot(residual, dv[lv], preferred_element_type=F32).astype(BF16)

            @pl.when(step < pairs)
            def _():
                mine = dd * ny + yy
                yg[item, mine] = value
                for share in shares:
                    here = yg.at[item, mine]
                    send(here, here, 3, item, share_peer(*share))

            zo[lv, :, columns(pn)] = value.astype(F32).T.astype(BF16)

            @pl.when(pn == PANELS - 1)
            def _():
                output(z_hbm, zo, 1, lv).start()

        @pl.when(step == 0)
        def _():
            finish(ft[lv * PANELS + pn])

        @pl.when(step > 0)
        def _():
            arrived(5, prev)
            acc0 = ownb[pn, 0:H]
            for k in range(nx - 1):
                acc0 = acc0 + lr[prev, 0, k].astype(F32)
            acc1 = ownb[pn, H:W]
            for k in range(nz - 1):
                acc1 = acc1 + lr[prev, 1, k].astype(F32)
            acc = jnp.concatenate([acc0, acc1], axis=0)
            finish((ft[lv * PANELS + pn].astype(F32) - acc).astype(BF16))

    def b3(item):
        lv = pairs - 1 - item // PANELS
        arrived(3, item)
        solved = jnp.concatenate([yg[item, k] for k in range(2 * ny)], axis=1)
        for at in range(nz):
            span = slice(at * nx * W, (at + 1) * nx * W)
            part = jnp.dot(solved, mv[lv, :, span], preferred_element_type=F32).astype(BF16)
            for j in range(nx):
                rs[item, at, j] = part[:, j * W : (j + 1) * W]
        for k in far_first(nz):
            at = (zz + k) % nz
            send(rs.at[item, at, :, 0:H], rr0.at[item, k - 1], 4, item, z_peer(k))
        for k in far_first(nx):
            at = (xx + k) % nx
            send(rs.at[item, :, at, H:W], rr1.at[item, k - 1], 4, item, x_peer(k))

    def b4(item):
        pn = item % PANELS
        arrived(4, item)
        for k in far_first(nx) + [0]:
            at = (xx + k) % nx
            acc = rs[item, zz, at, 0:H].astype(F32)
            for j in range(nz - 1):
                acc = acc + rr0[item, j, at].astype(F32)
            if k == 0:
                ownb[pn, 0:H] = acc
            else:
                ls[item, 0, k - 1] = acc.astype(BF16)
                send(ls.at[item, 0, k - 1], lr.at[item, 0, k - 1], 5, item, x_peer(k))
        for k in far_first(nz) + [0]:
            at = (zz + k) % nz
            acc = rs[item, at, xx, H:W].astype(F32)
            for j in range(nx - 1):
                acc = acc + rr1[item, j, at].astype(F32)
            if k == 0:
                ownb[pn, H:W] = acc
            else:
                ls[item, 1, k - 1] = acc.astype(BF16)
                send(ls.at[item, 1, k - 1], lr.at[item, 1, k - 1], 5, item, z_peer(k))

    def mask(lv):
        pltpu.make_async_copy(m_hbm.at[lv], mv.at[lv], load_sem.at[lv]).wait()
        cols = nz * nx * W
        spread = (
            lax.broadcasted_iota(jnp.int32, (nz * nx, cols), 1) // W
            == lax.broadcasted_iota(jnp.int32, (nz * nx, cols), 0)
        ).astype(BF16)
        gate = jnp.dot(
            pat_ref[lv].astype(F32).astype(BF16), spread, preferred_element_type=F32
        ).astype(BF16)
        for t in range(2 * ny):
            span = pl.ds(t * W, W)
            mv[lv, span, :] = mv[lv, span, :] * gate[t : t + 1, :]

    def settle(item, stages):
        for st in stages:
            sent(st, item)

    def stage(fn, index, count, *extra):
        @pl.when((index >= 0) & (index < count))
        def _():
            fn(index, *extra)

    def first(item, carry):
        f1(item)
        return carry

    def slot(s, carry):
        j = s - items

        @pl.when(s >= PANELS)
        def _():
            stage(f1, s, items + PANELS)

        stage(b4, j - 3, items)
        stage(b1, j, items + PANELS)
        stage(f2, s - 1, items)

        @pl.when((s % PANELS == 1) & (s < items))
        def _():
            mask(s // PANELS)

        @pl.when(s == 1)
        def _():
            for lv in range(1, levels):
                for copy in load_inputs(lv):
                    copy.wait()

        stage(f3, s - 2, items)
        stage(b3, j - 1, items)
        stage(settle, j - 1, items, (0, 1, 2))
        stage(settle, j - 5, items, (3, 4, 5))
        return carry

    lax.fori_loop(0, PANELS, first, 0)
    lax.fori_loop(1, 2 * items + PANELS, slot, 0)
    for item in range(items - 1, items):
        settle(item, (3, 4, 5))
    for lv in range(levels):
        output(f_hbm, fo, 0, lv).wait()
        output(z_hbm, zo, 1, lv).wait()


def body(nz, nx, ny, right_side, inverse_diag, coupling, pattern):
    levels, rhs = right_side.shape[0], right_side.shape[4]
    pairs = levels - 1
    items = pairs * PANELS
    rows, cols = coupling.shape[2], coupling.shape[4]
    b = right_side.reshape(levels, W, rhs)
    d = inverse_diag.reshape(levels, W, W)
    m = coupling.reshape(pairs, rows, cols)
    pat = pattern.reshape(pairs, 2 * ny, nz * nx)
    hbm = pl.BlockSpec(memory_space=pl.ANY)
    f, z = pl.pallas_call(
        functools.partial(kernel, nz, nx, ny, levels),
        out_shape=[jax.ShapeDtypeStruct((levels, W, rhs), BF16)] * 2,
        in_specs=[hbm, hbm, pl.BlockSpec(memory_space=pltpu.VMEM), hbm],
        out_specs=[hbm, hbm],
        scratch_shapes=[
            pltpu.VMEM((levels, W, rhs), BF16),
            pltpu.VMEM((levels, W, W), BF16),
            pltpu.VMEM((levels, W, rhs), BF16),
            pltpu.VMEM((levels, W, rhs), BF16),
            pltpu.VMEM((pairs, rows, cols), BF16),
            pltpu.VMEM((items, nz, nx, W, W), BF16),
            pltpu.VMEM((PANELS, W, W), F32),
            pltpu.VMEM((items, 2 * ny - 1, W, W), BF16),
            pltpu.VMEM((items, 2 * ny - 1, W, W), BF16),
            pltpu.VMEM((items, 2 * ny, W, W), BF16),
            pltpu.VMEM((items, nz, nx, W, W), BF16),
            pltpu.VMEM((items, nz - 1, nx, H, W), BF16),
            pltpu.VMEM((items, nx - 1, nz, H, W), BF16),
            pltpu.VMEM((items, 2, nx - 1, H, W), BF16),
            pltpu.VMEM((items, 2, nx - 1, H, W), BF16),
            pltpu.VMEM((PANELS, W, W), F32),
            pltpu.VMEM((items + PANELS, W, W), BF16),
            pltpu.SemaphoreType.DMA((pairs,)),
            pltpu.SemaphoreType.DMA((2, levels)),
            pltpu.SemaphoreType.DMA((2, levels)),
            pltpu.SemaphoreType.DMA((6, items)),
            pltpu.SemaphoreType.DMA((6, items)),
        ],
        compiler_params=pltpu.CompilerParams(
            collective_id=0, has_side_effects=True, vmem_limit_bytes=60 * 1024 * 1024
        ),
    )(b, d, pat, m)
    shape = right_side.shape
    return f.reshape(shape), z.reshape(shape)


def solution(mesh):
    placed = (
        P(None, "row", ("depth", "col"), None, None),
        P(None, "row", ("depth", "col"), None, None, None),
        P(None, "row", None, ("depth", "col"), None),
        P(None, "row", None, ("depth", "col"), None),
    )
    side = round(mesh.shape["row"] ** 0.5)
    return jax.shard_map(
        functools.partial(body, side, side, mesh.shape["col"]),
        mesh=mesh,
        in_specs=placed,
        out_specs=(placed[0], placed[0]),
        check_vma=False,
    )
```

time: 136 us -> 127 us (0.934)
  Pallas kernels: 130 us -> 122 us
    pallas_call x1, Pallas kernels: 130 us -> 122 us  [body(): pl.pallas_call(functools.partial(kernel, nz, nx, ny, levels), out_shape=[...]
where the time goes in v2:
time: 127 us; the launch traced here: 126 us
  Pallas kernels  122 us (96%)
  local copies, waits for them, and re-layouts  3.74 us (3%)
    pallas_call x1, Pallas kernels, body(): pl.pallas_call(functools.partial(kernel, nz, nx, ny, levels), out_shape=[...  122 us
    unnamed x2, local copies, waits for them, and re-layouts  3.74 us

profile of v2, /device:TPU:0, one launch (start us, length us, event | category | flops | bytes accessed | tf_op | source)
XLA Modules:
  0.0 126.4 jit_solution(1548719007838600560)
XLA Ops:
  0.6 122.0 %shard_map.59 = (bf16[4,128,512]{2,1,0:T(8,128)(2,1)}, bf16[4,128,512]{2,1,0:T(8,128)(2,1)}) custom-call(bf16[4,128,512]{2,1,0:T(8,128)(2,1)} %bitcast.13, bf16[4,128,128]{2,1,0:T(8,128)(2,1)} %bitcast.14, s32[3,8,16]{2,1,0:T(8,128)} %bitcast.15, bf16[3,1024,2048]{2,1,0:T(8,128)(2,1)} %bitcast.10), custom_call_target="tpu_custom_call" | custom-call | tf_op jit(solution)/shard_map/pallas_call | solution.py:326
  122.7 1.9 %copy.10 = bf16[4,1,1,128,512]{4,3,2,1,0:T(8,128)(2,1)} copy(bf16[4,1,1,128,512]{4,3,2,1,0:T(8,128)(2,1)} %bitcast.12) | data formatting | bytes 1048576
  124.5 1.9 %copy.11 = bf16[4,1,1,128,512]{4,3,2,1,0:T(8,128)(2,1)} copy(bf16[4,1,1,128,512]{4,3,2,1,0:T(8,128)(2,1)} %bitcast.11) | data formatting | bytes 1048576

commit v3 on v2

--- a/solution.py
+++ b/solution.py
@@ -20,10 +20,10 @@
 
 def kernel(
     nz, nx, ny, levels,
-    b_hbm, d_hbm, pat_ref, m_hbm,
-    f_hbm, z_hbm,
-    bv, dv, fo, zo, mv, xg, ownf, ys, yr, yg, rs, rr0, rr1, ls, lr, ownb, ft,
-    load_sem, in_sem, out_sem, send_sem, recv_sem,
+    b_hbm, d_hbm, pat_hbm, m_hbm,
+    fo, zo,
+    bv, dv, pat, gate, mv, mt, xg, ownf, yf, ys, yr, yg, rs, rr0, rr1, ls, lr, ownb, ft,
+    load_sem, in_sem, pat_sem, send_sem, recv_sem,
 ):
     pairs = levels - 1
     items = pairs * PANELS
@@ -55,17 +55,22 @@
             barrier, inc=1, device_id=peer, device_id_type=pl.DeviceIdType.MESH
         )
 
+    def load_coupling(lv):
+        return pltpu.make_async_copy(m_hbm.at[lv], mv.at[lv], load_sem.at[lv])
+
     def load_inputs(lv):
         return (
             pltpu.make_async_copy(b_hbm.at[lv], bv.at[lv], in_sem.at[0, lv]),
             pltpu.make_async_copy(d_hbm.at[lv], dv.at[lv], in_sem.at[1, lv]),
         )
 
+    load_pattern = pltpu.make_async_copy(pat_hbm, pat, pat_sem)
+    load_pattern.start()
     for lv in range(levels):
         for copy in load_inputs(lv):
             copy.start()
         if lv < pairs:
-            pltpu.make_async_copy(m_hbm.at[lv], mv.at[lv], load_sem.at[lv]).start()
+            load_coupling(lv).start()
 
     for copy in load_inputs(0):
         copy.wait()
@@ -102,15 +107,14 @@
     def columns(panel):
         return pl.ds(pl.multiple_of(panel * W, W), W)
 
-    def output(hbm, buf, which, lv):
-        return pltpu.make_async_copy(buf.at[lv], hbm.at[lv], out_sem.at[which, lv])
-
     def f1(item):
         lv, pn = item // PANELS, item % PANELS
         prev = item - PANELS
 
         def finish(residual):
-            value = jnp.dot(dv[lv], residual, preferred_element_type=F32).astype(BF16)
+            value = lax.dot_general(
+                residual, dv[lv], (((1,), (1,)), ((), ())), preferred_element_type=F32
+            ).astype(BF16)
 
             @pl.when(lv < pairs)
             def _():
@@ -122,16 +126,14 @@
                     here = xg.at[item, zz, xx, H:W]
                     send(here, here, 0, item, z_peer(k))
 
-            fo[lv, :, columns(pn)] = value
-            ft[item] = value.astype(F32).T.astype(BF16)
-
-            @pl.when(pn == PANELS - 1)
-            def _():
-                output(f_hbm, fo, 0, lv).start()
+            ft[item] = value
+            fo[lv, :, columns(pn)] = value.astype(F32).T.astype(BF16)
+
+        given = bv[lv, :, columns(pn)].astype(F32).T
 
         @pl.when(lv == 0)
         def _():
-            finish(bv[0, :, columns(pn)])
+            finish(given.astype(BF16))
 
         @pl.when(lv > 0)
         def _():
@@ -139,7 +141,7 @@
             acc = ownf[pn]
             for k in range(2 * ny - 1):
                 acc = acc + yr[prev, k].astype(F32)
-            finish((bv[lv, :, columns(pn)].astype(F32) - acc).astype(BF16))
+            finish((given - acc).astype(BF16))
 
     def f2(item):
         arrived(0, item)
@@ -152,25 +154,30 @@
 
     def f3(item):
         lv, pn = item // PANELS, item % PANELS
+
+        @pl.when(item >= PANELS)
+        def _():
+            sent(2, item - PANELS)
+
         arrived(1, item)
-        gathered = xg[item].reshape(nz * nx * W, W)
-        for k in far_first(ny) + [0]:
-            at = (yy + k) % ny
-            rows = [
-                mv[lv, pl.ds(pl.multiple_of((side * ny + at) * W, W), W), :]
-                for side in (dd, (dd + 1) % 2)
-            ]
-            part = jnp.dot(
-                jnp.concatenate(rows, axis=0), gathered, preferred_element_type=F32
-            )
-            for flip in (0, 1):
-                block = part[flip * W : (flip + 1) * W]
-                if flip == 0 and k == 0:
-                    ownf[pn] = block
-                else:
-                    slot = flip * ny + k - 1
-                    ys[item, slot] = block.astype(BF16)
-                    send(ys.at[item, slot], yr.at[item, slot], 2, item, share_peer(flip, k))
+        solved = jnp.concatenate(
+            [xg[item, i, j] for i in range(nz) for j in range(nx)], axis=1
+        )
+        for side in (0, 1):
+            span = slice(side * ny * W, (side + 1) * ny * W)
+            part = jnp.dot(solved, mt[lv, :, span], preferred_element_type=F32)
+            for j in range(ny):
+                yf[side * ny + j] = part[:, j * W : (j + 1) * W]
+            for k in far_first(ny):
+                slot = (dd + side) % 2 * ny + k - 1
+                ys[pn, slot] = yf[side * ny + (yy + k) % ny].astype(BF16)
+                send(
+                    ys.at[pn, slot], yr.at[item, slot], 2, item,
+                    share_peer((dd + side) % 2, k),
+                )
+        ys[pn, ny - 1] = yf[(1 - dd) * ny + yy].astype(BF16)
+        send(ys.at[pn, ny - 1], yr.at[item, ny - 1], 2, item, share_peer(1, 0))
+        ownf[pn] = yf[dd * ny + yy]
 
     def b1(item):
         step, pn = item // PANELS, item % PANELS
@@ -184,15 +191,13 @@
             def _():
                 mine = dd * ny + yy
                 yg[item, mine] = value
-                for share in shares:
-                    here = yg.at[item, mine]
-                    send(here, here, 3, item, share_peer(*share))
+                here = yg.at[item, mine]
+                for k in far_first(ny):
+                    for side in (0, 1):
+                        send(here, here, 3, item, share_peer((dd + side) % 2, k))
+                send(here, here, 3, item, share_peer(1, 0))
 
             zo[lv, :, columns(pn)] = value.astype(F32).T.astype(BF16)
-
-            @pl.when(pn == PANELS - 1)
-            def _():
-                output(z_hbm, zo, 1, lv).start()
 
         @pl.when(step == 0)
         def _():
@@ -211,27 +216,32 @@
             finish((ft[lv * PANELS + pn].astype(F32) - acc).astype(BF16))
 
     def b3(item):
-        lv = pairs - 1 - item // PANELS
+        lv, pn = pairs - 1 - item // PANELS, item % PANELS
+
+        @pl.when(item >= PANELS)
+        def _():
+            sent(4, item - PANELS)
+
         arrived(3, item)
         solved = jnp.concatenate([yg[item, k] for k in range(2 * ny)], axis=1)
         for at in range(nz):
             span = slice(at * nx * W, (at + 1) * nx * W)
             part = jnp.dot(solved, mv[lv, :, span], preferred_element_type=F32).astype(BF16)
             for j in range(nx):
-                rs[item, at, j] = part[:, j * W : (j + 1) * W]
+                rs[pn, at, j] = part[:, j * W : (j + 1) * W]
         for k in far_first(nz):
             at = (zz + k) % nz
-            send(rs.at[item, at, :, 0:H], rr0.at[item, k - 1], 4, item, z_peer(k))
+            send(rs.at[pn, at, :, 0:H], rr0.at[item, k - 1], 4, item, z_peer(k))
         for k in far_first(nx):
             at = (xx + k) % nx
-            send(rs.at[item, :, at, H:W], rr1.at[item, k - 1], 4, item, x_peer(k))
+            send(rs.at[pn, :, at, H:W], rr1.at[item, k - 1], 4, item, x_peer(k))
 
     def b4(item):
         pn = item % PANELS
         arrived(4, item)
         for k in far_first(nx) + [0]:
             at = (xx + k) % nx
-            acc = rs[item, zz, at, 0:H].astype(F32)
+            acc = rs[pn, zz, at, 0:H].astype(F32)
             for j in range(nz - 1):
                 acc = acc + rr0[item, j, at].astype(F32)
             if k == 0:
@@ -241,7 +251,7 @@
                 send(ls.at[item, 0, k - 1], lr.at[item, 0, k - 1], 5, item, x_peer(k))
         for k in far_first(nz) + [0]:
             at = (zz + k) % nz
-            acc = rs[item, at, xx, H:W].astype(F32)
+            acc = rs[pn, at, xx, H:W].astype(F32)
             for j in range(nx - 1):
                 acc = acc + rr1[item, j, at].astype(F32)
             if k == 0:
@@ -250,19 +260,26 @@
                 ls[item, 1, k - 1] = acc.astype(BF16)
                 send(ls.at[item, 1, k - 1], lr.at[item, 1, k - 1], 5, item, z_peer(k))
 
-    def mask(lv):
-        pltpu.make_async_copy(m_hbm.at[lv], mv.at[lv], load_sem.at[lv]).wait()
+    def spread_pattern():
         cols = nz * nx * W
         spread = (
             lax.broadcasted_iota(jnp.int32, (nz * nx, cols), 1) // W
             == lax.broadcasted_iota(jnp.int32, (nz * nx, cols), 0)
         ).astype(BF16)
-        gate = jnp.dot(
-            pat_ref[lv].astype(F32).astype(BF16), spread, preferred_element_type=F32
-        ).astype(BF16)
-        for t in range(2 * ny):
-            span = pl.ds(t * W, W)
-            mv[lv, span, :] = mv[lv, span, :] * gate[t : t + 1, :]
+        for lv in range(pairs):
+            rows = jnp.dot(
+                pat[lv].astype(F32).astype(BF16), spread, preferred_element_type=F32
+            )
+            for t in range(2 * ny):
+                gate[lv, t] = rows[t : t + 1, :]
+
+    def mask(lv, quarter):
+        for t in range(2 * ny // 4):
+            row = quarter * (2 * ny // 4) + t
+            span = pl.ds(pl.multiple_of(row * W, W), W)
+            gated = mv[lv, span, :] * gate[lv, row].astype(BF16)
+            mv[lv, span, :] = gated
+            mt[lv, :, span] = gated.T
 
     def settle(item, stages):
         for st in stages:
@@ -288,29 +305,48 @@
         stage(b1, j, items + PANELS)
         stage(f2, s - 1, items)
 
-        @pl.when((s % PANELS == 1) & (s < items))
-        def _():
-            mask(s // PANELS)
+        ahead = s + PANELS - 2
+
+        @pl.when((ahead >= PANELS) & (ahead < items))
+        def _():
+            @pl.when(ahead % PANELS == 0)
+            def _():
+                load_coupling(ahead // PANELS).wait()
+
+            mask(ahead // PANELS, ahead % PANELS)
 
         @pl.when(s == 1)
         def _():
-            for lv in range(1, levels):
-                for copy in load_inputs(lv):
-                    copy.wait()
+            load_coupling(0).wait()
+            for quarter in range(4):
+                mask(0, quarter)
 
         stage(f3, s - 2, items)
         stage(b3, j - 1, items)
-        stage(settle, j - 1, items, (0, 1, 2))
-        stage(settle, j - 5, items, (3, 4, 5))
+        stage(settle, j - 1, items, (0, 1))
+        stage(settle, j - 5, items, (3, 5))
         return carry
 
     lax.fori_loop(0, PANELS, first, 0)
+    load_pattern.wait()
+    spread_pattern()
+    for lv in range(1, levels):
+        for copy in load_inputs(lv):
+            copy.wait()
     lax.fori_loop(1, 2 * items + PANELS, slot, 0)
-    for item in range(items - 1, items):
-        settle(item, (3, 4, 5))
-    for lv in range(levels):
-        output(f_hbm, fo, 0, lv).wait()
-        output(z_hbm, zo, 1, lv).wait()
+    settle(items - 1, (3, 5))
+    for item in range(items - PANELS, items):
+        settle(item, (2, 4))
+
+def store(f_in, z_in, f_out, z_out, sem):
+    copies = (
+        pltpu.make_async_copy(f_in, f_out, sem.at[0]),
+        pltpu.make_async_copy(z_in, z_out, sem.at[1]),
+    )
+    for copy in copies:
+        copy.start()
+    for copy in copies:
+        copy.wait()
 
 
 def body(nz, nx, ny, right_side, inverse_diag, coupling, pattern):
@@ -321,25 +357,29 @@
     b = right_side.reshape(levels, W, rhs)
     d = inverse_diag.reshape(levels, W, W)
     m = coupling.reshape(pairs, rows, cols)
-    pat = pattern.reshape(pairs, 2 * ny, nz * nx)
-    hbm = pl.BlockSpec(memory_space=pl.ANY)
+    gate = pattern.reshape(pairs, 2 * ny, nz * nx)
+    hbm = pl.BlockSpec(memory_space=pltpu.HBM)
+    vm = pl.BlockSpec(memory_space=pltpu.VMEM)
+    b, d, gate = (pltpu.with_memory_space_constraint(x, pltpu.HBM) for x in (b, d, gate))
     f, z = pl.pallas_call(
         functools.partial(kernel, nz, nx, ny, levels),
         out_shape=[jax.ShapeDtypeStruct((levels, W, rhs), BF16)] * 2,
-        in_specs=[hbm, hbm, pl.BlockSpec(memory_space=pltpu.VMEM), hbm],
-        out_specs=[hbm, hbm],
+        in_specs=[hbm, hbm, hbm, hbm],
+        out_specs=[vm, vm],
         scratch_shapes=[
             pltpu.VMEM((levels, W, rhs), BF16),
             pltpu.VMEM((levels, W, W), BF16),
-            pltpu.VMEM((levels, W, rhs), BF16),
-            pltpu.VMEM((levels, W, rhs), BF16),
+            pltpu.VMEM((pairs, 2 * ny, nz * nx), jnp.int32),
+            pltpu.VMEM((pairs, 2 * ny, 1, cols), F32),
             pltpu.VMEM((pairs, rows, cols), BF16),
+            pltpu.VMEM((pairs, cols, rows), BF16),
             pltpu.VMEM((items, nz, nx, W, W), BF16),
             pltpu.VMEM((PANELS, W, W), F32),
-            pltpu.VMEM((items, 2 * ny - 1, W, W), BF16),
+            pltpu.VMEM((2 * ny, W, W), F32),
+            pltpu.VMEM((PANELS, 2 * ny - 1, W, W), BF16),
             pltpu.VMEM((items, 2 * ny - 1, W, W), BF16),
             pltpu.VMEM((items, 2 * ny, W, W), BF16),
-            pltpu.VMEM((items, nz, nx, W, W), BF16),
+            pltpu.VMEM((PANELS, nz, nx, W, W), BF16),
             pltpu.VMEM((items, nz - 1, nx, H, W), BF16),
             pltpu.VMEM((items, nx - 1, nz, H, W), BF16),
             pltpu.VMEM((items, 2, nx - 1, H, W), BF16),
@@ -348,15 +388,24 @@
             pltpu.VMEM((items + PANELS, W, W), BF16),
             pltpu.SemaphoreType.DMA((pairs,)),
             pltpu.SemaphoreType.DMA((2, levels)),
-            pltpu.SemaphoreType.DMA((2, levels)),
+            pltpu.SemaphoreType.DMA,
             pltpu.SemaphoreType.DMA((6, items)),
             pltpu.SemaphoreType.DMA((6, items)),
         ],
         compiler_params=pltpu.CompilerParams(
-            collective_id=0, has_side_effects=True, vmem_limit_bytes=60 * 1024 * 1024
+            collective_id=0, has_side_effects=True, vmem_limit_bytes=50 * 1024 * 1024
         ),
-    )(b, d, pat, m)
+    )(b, d, gate, m)
     shape = right_side.shape
+    anywhere = pl.BlockSpec(memory_space=pl.ANY)
+    f, z = pl.pallas_call(
+        store,
+        out_shape=[jax.ShapeDtypeStruct((levels, W, rhs), BF16)] * 2,
+        in_specs=[anywhere, anywhere],
+        out_specs=[anywhere, anywhere],
+        scratch_shapes=[pltpu.SemaphoreType.DMA((2,))],
+        compiler_params=pltpu.CompilerParams(vmem_limit_bytes=50 * 1024 * 1024),
+    )(f, z)
     return f.reshape(shape), z.reshape(shape)
 
 

time: 127 us -> 122 us (0.961)
  local copies, waits for them, and re-layouts: 3.74 us -> 0 us
    unnamed x2 -> x0, local copies, waits for them, and re-layouts: 3.74 us -> none
    pallas_call x1, Pallas kernels: 122 us -> 120 us  [body(): pl.pallas_call(functools.partial(kernel, nz, nx, ny, levels), out_shape=[...]
where the time goes in v3:
time: 122 us
  Pallas kernels  121 us (99%)
    pallas_call x1, Pallas kernels, body(): pl.pallas_call(functools.partial(kernel, nz, nx, ny, levels), out_shape=[...  120 us

profile of v3, /device:TPU:0, one launch (start us, length us, event | category | flops | bytes accessed | tf_op | source)
XLA Modules:
  0.0 122.1 jit_solution(3573295697741392136)
XLA Ops:
  0.6 120.5 %shard_map.59 = (bf16[4,128,512]{2,1,0:T(8,128)(2,1)S(1)}, bf16[4,128,512]{2,1,0:T(8,128)(2,1)S(1)}) custom-call(bf16[4,128,512]{2,1,0:T(8,128)(2,1)} %bitcast.11, bf16[4,128,128]{2,1,0:T(8,128)(2,1)} %bitcast.12, s32[3,8,16]{2,1,0:T(8,128)} %bitcast.13, bf16[3,1024,2048]{2,1,0:T(8,128)(2,1)} %bitcast.10), custom_call_target="tpu_custom_call" | custom-call | tf_op jit(solution)/shard_map/pallas_call | solution.py:364
  121.1 1.0 shard_map.60

commit v4 on v3

--- a/solution.py
+++ b/solution.py
@@ -294,16 +294,23 @@
         f1(item)
         return carry
 
+    def second(item, carry):
+        f2(item)
+        return carry
+
     def slot(s, carry):
         j = s - items
 
+        stage(b4, j - 3, items)
         @pl.when(s >= PANELS)
         def _():
             stage(f1, s, items + PANELS)
 
-        stage(b4, j - 3, items)
         stage(b1, j, items + PANELS)
-        stage(f2, s - 1, items)
+        @pl.when(s > PANELS)
+        def _():
+            stage(f2, s - 1, items)
+
 
         ahead = s + PANELS - 2
 
@@ -317,6 +324,7 @@
 
         @pl.when(s == 1)
         def _():
+            lax.fori_loop(0, PANELS, second, 0)
             load_coupling(0).wait()
             for quarter in range(4):
                 mask(0, quarter)

time: 122 us -> 121 us (level)
    pallas_call x1, Pallas kernels: 120 us -> 119 us  [body(): pl.pallas_call(functools.partial(kernel, nz, nx, ny, levels), out_shape=[...]
where the time goes in v4:
time: 121 us
  Pallas kernels  120 us (99%)
    pallas_call x1, Pallas kernels, body(): pl.pallas_call(functools.partial(kernel, nz, nx, ny, levels), out_shape=[...  119 us

profile of v4, /device:TPU:0, one launch (start us, length us, event | category | flops | bytes accessed | tf_op | source)
XLA Modules:
  0.0 120.7 jit_solution(16590144775182748437)
XLA Ops:
  0.6 119.1 %shard_map.59 = (bf16[4,128,512]{2,1,0:T(8,128)(2,1)S(1)}, bf16[4,128,512]{2,1,0:T(8,128)(2,1)S(1)}) custom-call(bf16[4,128,512]{2,1,0:T(8,128)(2,1)} %bitcast.11, bf16[4,128,128]{2,1,0:T(8,128)(2,1)} %bitcast.12, s32[3,8,16]{2,1,0:T(8,128)} %bitcast.13, bf16[3,1024,2048]{2,1,0:T(8,128)(2,1)} %bitcast.10), custom_call_target="tpu_custom_call" | custom-call | tf_op jit(solution)/shard_map/pallas_call | solution.py:372
  119.7 1.0 shard_map.60

commit v5 on v4

--- a/solution.py
+++ b/solution.py
@@ -65,15 +65,17 @@
         )
 
     load_pattern = pltpu.make_async_copy(pat_hbm, pat, pat_sem)
+    for copy in load_inputs(0):
+        copy.start()
     load_pattern.start()
-    for lv in range(levels):
+    for copy in load_inputs(0):
+        copy.wait()
+    for lv in range(1, levels):
         for copy in load_inputs(lv):
             copy.start()
-        if lv < pairs:
-            load_coupling(lv).start()
-
-    for copy in load_inputs(0):
-        copy.wait()
+    for lv in range(pairs):
+        load_coupling(lv).start()
+
     pl.semaphore_wait(barrier, len(peers))
 
     def send(src, dst, stage, item, peer):
@@ -301,7 +303,10 @@
     def slot(s, carry):
         j = s - items
 
-        stage(b4, j - 3, items)
+        @pl.when(j <= items)
+        def _():
+            stage(b4, j - 3, items)
+
         @pl.when(s >= PANELS)
         def _():
             stage(f1, s, items + PANELS)
@@ -331,6 +336,11 @@
 
         stage(f3, s - 2, items)
         stage(b3, j - 1, items)
+
+        @pl.when(j >= items)
+        def _():
+            stage(b4, j - 2, items)
+
         stage(settle, j - 1, items, (0, 1))
         stage(settle, j - 5, items, (3, 5))
         return carry

time: 121 us -> 121 us (level)
  no operation moved by 1% of the time
where the time goes in v5:
time: 121 us
  Pallas kernels  120 us (99%)
    pallas_call x1, Pallas kernels, body(): pl.pallas_call(functools.partial(kernel, nz, nx, ny, levels), out_shape=[...  119 us

profile of v5, /device:TPU:0, one launch (start us, length us, event | category | flops | bytes accessed | tf_op | source)
XLA Modules:
  0.0 120.9 jit_solution(3921526550863861637)
XLA Ops:
  0.6 119.3 %shard_map.59 = (bf16[4,128,512]{2,1,0:T(8,128)(2,1)S(1)}, bf16[4,128,512]{2,1,0:T(8,128)(2,1)S(1)}) custom-call(bf16[4,128,512]{2,1,0:T(8,128)(2,1)} %bitcast.11, bf16[4,128,128]{2,1,0:T(8,128)(2,1)} %bitcast.12, s32[3,8,16]{2,1,0:T(8,128)} %bitcast.13, bf16[3,1024,2048]{2,1,0:T(8,128)(2,1)} %bitcast.10), custom_call_target="tpu_custom_call" | custom-call | tf_op jit(solution)/shard_map/pallas_call | solution.py:382
  119.9 1.0 shard_map.60
